TPU v7x, 256 devices: a whole 4x4x8 slice. The times are simulated.
256 devices in a mesh: dp: 8 (over x, core), tensor: 32 (over z, y).
Axes of the slice: x: 4, y: 4, z: 8, core: 2. Of those that a mesh axis runs over, the one named last changes fastest.
Arguments:
- hidden: bfloat16 [6144, 4096], P('dp', 'tensor'), may hold values from -2000 to 2000
- out_embed: bfloat16 [65536, 4096], P('tensor', 'dp'), may hold values from -0.3 to 0.3
- labels: int32 [6144], P('dp'), may hold values from 0 to 65535
Outputs:
- token_loss: float32 [6144], P(('dp', 'tensor'))
- mean_loss: float32 [], replicated
All inputs are finite; a program needn't handle non-finite values.
Results may differ from a plain program's by a relative error of at most 0.0003.
Values may be sent and summed in bfloat16 or wider, within the bound.
A program may use at most 128 MiB of HBM per device.

v0:
```python
import jax
import jax.numpy as jnp
from jax import lax
from jax.sharding import Mesh
from jax.sharding import PartitionSpec as P

BLOCK = 512
TENSOR = ("tensor_0", "tensor_1")
DP = ("dp_0", "dp_1")
DP_TENSOR = ("dp_0", "dp_1", "tensor_0", "tensor_1")


def whole_of(shard, axes, dim):
    for axis in reversed(axes):
        shard = lax.all_gather(shard, axis, axis=dim, tiled=True)
    return shard


def side_by_side(arrays, axis, split_dim, concat_dim, along):
    both = jnp.concatenate(arrays, axis=along)
    filled, at, done = (
        lax.all_to_all(both, axis, split_axis=split_dim, concat_axis=concat_dim, tiled=True),
        0,
        [],
    )
    for a in arrays:
        done.append(lax.slice_in_dim(filled, at, at + a.shape[along], axis=along))
        at += a.shape[along]
    return tuple(done)


def one_axis_at_a_time(shard, axes):
    for axis in axes:
        shard = lax.psum(shard, axis)
    return shard


def combine_stats(first, second):
    peak_first, mass_first, label_first = first
    peak_second, mass_second, label_second = second
    peak_value = jnp.maximum(peak_first, peak_second)
    exp_total = mass_first * jnp.exp(peak_first - peak_value) + mass_second * jnp.exp(
        peak_second - peak_value
    )
    return (peak_value, exp_total, label_first + label_second)


def block_stats(logits, first_row, labels):
    peak_value = jnp.max(logits, axis=0)
    exp_total = jnp.sum(jnp.exp(logits - peak_value[None, :]), axis=0)
    row_ids = first_row + lax.broadcasted_iota(jnp.int32, logits.shape, 0)
    label_logit = jnp.sum(
        jnp.where(row_ids == labels[None, :], logits, jnp.zeros_like(logits)), axis=0
    )
    return (peak_value, exp_total, label_logit)


def body(hidden, out_embed, labels):
    full_hidden = whole_of(hidden, TENSOR, 1)
    token_count = full_hidden.shape[0]
    vocab_rows = out_embed.shape[0]
    vocab_offset = lax.axis_index(TENSOR) * vocab_rows
    block_count = vocab_rows // BLOCK
    all_logits = lax.dot_general(
        lax.all_gather(out_embed, DP, axis=1, tiled=True),
        full_hidden,
        (((1,), (1,)), ((), ())),
        preferred_element_type=jnp.float32,
    )
    running_stats = None
    for block_index in range(block_count):
        stats = block_stats(
            all_logits[block_index * BLOCK : (block_index + 1) * BLOCK],
            vocab_offset + block_index * BLOCK,
            labels,
        )
        running_stats = stats if running_stats is None else combine_stats(running_stats, stats)
    groups = lax.axis_size(TENSOR)
    share = token_count // groups
    peak_all, mass_all, label_all = running_stats
    peaks, masses, picked = side_by_side(
        (
            peak_all.reshape(groups, share),
            mass_all.reshape(groups, share),
            label_all.reshape(groups, share),
        ),
        TENSOR,
        0,
        0,
        1,
    )
    peak_value = jnp.max(peaks, axis=0)
    exp_total = jnp.sum(masses * jnp.exp(peaks - peak_value[None, :]), axis=0)
    label_logit = jnp.sum(picked, axis=0)
    token_loss = jnp.log(exp_total) + peak_value - label_logit
    loss_sum = one_axis_at_a_time(jnp.sum(token_loss), DP_TENSOR)
    mean_loss = loss_sum / (share * lax.axis_size(DP) * groups)
    return (token_loss, mean_loss)


def solution(mesh):
    finer = Mesh(mesh.devices.reshape(4, 2, 8, 4), ("dp_0", "dp_1", "tensor_0", "tensor_1"))
    return jax.shard_map(
        body,
        mesh=finer,
        in_specs=(P(DP, TENSOR), P(TENSOR, DP), P(DP)),
        out_specs=(P(DP_TENSOR), P()),
        check_vma=False,
    )
```

profile of v0, /device:TPU:32, one launch (start us, length us, event | category | flops | bytes accessed | tf_op | source)
XLA Modules:
  0.0 282.1 jit_solution(3417769360817746753)
XLA Ops:
  7.2 0.0 all-gather.5.cloned.1.call-start
  7.2 18.9 %all_gather.10 = bf16[768,512]{1,0:T(8,128)(2,1)} all-gather(bf16[768,128]{1,0:T(8,128)(2,1)} %param.3), channel_id=1, replica_groups=mesh['dp_0'=4,'dp_1'=2,'tensor_0'=8,'tensor_1'=4] {'tensor_1'}, dimensions={1}, use_global_device_ids=true | all-gather | bytes 983040 | tf_op jit(solution)/shard_map/all_gather | solution.py:15
  26.1 0.0 all-gather.5.cloned.1.call-update
  26.2 0.0 all-gather.3.cloned.1.call-start
  26.2 0.7 all-gather.3.cloned.1.call-update
  27.0 73.0 %all-gather.5.cloned.1.call-done = bf16[768,4096]{1,0:T(8,128)(2,1)} async-done(((bf16[768,512]{1,0:T(8,128)(2,1)}), bf16[768,4096]{1,0:T(8,128)(2,1)}) %all-gather.5.cloned.1.call-update) | async-done | bytes 6291472 | tf_op jit(solution)/shard_map/all_gather | solution.py:15
  100.0 89.7 %all-gather.3.cloned.1.call-done = bf16[2048,4096]{1,0:T(8,128)(2,1)} async-done(((bf16[2048,512]{1,0:T(8,128)(2,1)}), bf16[2048,4096]{1,0:T(8,128)(2,1)}) %all-gather.3.cloned.1.call-update) | async-done | bytes 16777232 | tf_op jit(solution)/shard_map/all_gather | solution.py:65
  189.7 18.3 %fusion.3 = f32[2048,768]{1,0:T(8,128)S(1)} fusion(bf16[2048,4096]{1,0:T(8,128)(2,1)} %all-gather.3.cloned.1.call-done, bf16[768,4096]{1,0:T(8,128)(2,1)} %all-gather.5.cloned.1.call-done), kind=kOutput, calls=%fused_computation.26 | convolution fusion | flops 12884901888 | bytes 29360128 | tf_op jit(solution)/shard_map/dot_general | solution.py:64
  208.0 0.0 copy-start
  208.0 0.0 copy-start.1
  208.0 0.3 slice_reduce_fusion.1
  208.3 2.3 copy-done
  210.7 0.1 reduce_max.60
  210.7 0.1 reduce_max.58
  210.8 0.1 reduce_max.54
  210.9 0.1 reduce_max.56
  211.0 0.0 copy-done.1
  211.0 3.7 %exponential_reduce_fusion.3 = (f32[768]{0:T(1024)S(1)}, f32[768]{0:T(1024)S(1)}, f32[768]{0:T(1024)S(1)}, f32[768]{0:T(1024)S(1)}, f32[768]{0:T(1024)S(1)}, /*i...) fusion(f32[2048,768]{1,0:T(8,128)} %copy-done, f32[768]{0:T(1024)S(1)} %get-tuple-element.17, ...), kind=kLoop, calls=%fused_computation.7 | loop fusion | flops 7858176 | bytes 6339584 | tf_op jit(solution)/shard_map/reduce_sum | solution.py:50
  214.7 0.1 add.98
  214.8 0.1 reduce_sum.114
  214.9 0.1 reduce_sum.112
  215.0 0.1 reduce_sum.110
  215.0 0.1 reduce_sum.108
  215.2 0.1 pad_maximum_fusion
  215.3 18.5 %all_to_all.12 = f32[32,1,72]{2,1,0:T(1,128)S(1)} all-to-all(f32[32,1,72]{2,1,0:T(1,128)S(1)} %bitcast.8), channel_id=1, replica_groups=mesh['dp_0'=4,'dp_1'=2,'tensor_0'=8,'tensor_1'=4] {'tensor_0','tensor_1'}, dimensions={0} | all-to-all | bytes 18432 | tf_op jit(solution)/shard_map/all_to_all | solution.py:22
  233.8 0.1 fusion
  233.9 1.1 fusion.1
  235.0 9.8 %psum.28 = f32[]{:T(128)} all-reduce(f32[]{:T(128)} %get-tuple-element.20), channel_id=1, replica_groups=mesh['dp_0'=4,'dp_1'=2,'tensor_0'=8,'tensor_1'=4] {'dp_0'}, use_global_device_ids=true, to_apply=%region_16.17 | all-reduce | flops 1 | bytes 8 | tf_op jit(solution)/shard_map/psum | solution.py:34
  244.8 3.1 %psum.29 = f32[]{:T(128)} all-reduce(f32[]{:T(128)} %psum.28), channel_id=1, replica_groups=mesh['dp_0'=4,'dp_1'=2,'tensor_0'=8,'tensor_1'=4] {'dp_1'}, use_global_device_ids=true, to_apply=%region_17.18 | all-reduce | flops 1 | bytes 8 | tf_op jit(solution)/shard_map/psum | solution.py:34
  247.8 16.1 %psum.30 = f32[]{:T(128)} all-reduce(f32[]{:T(128)} %psum.29), channel_id=1, replica_groups=mesh['dp_0'=4,'dp_1'=2,'tensor_0'=8,'tensor_1'=4] {'tensor_0'}, use_global_device_ids=true, to_apply=%region_18.19 | all-reduce | flops 1 | bytes 8 | tf_op jit(solution)/shard_map/psum | solution.py:34
  264.0 9.6 %psum.31 = f32[]{:T(128)} all-reduce(f32[]{:T(128)} %psum.30), channel_id=1, replica_groups=mesh['dp_0'=4,'dp_1'=2,'tensor_0'=8,'tensor_1'=4] {'tensor_1'}, use_global_device_ids=true, to_apply=%region_19.20 | all-reduce | flops 1 | bytes 8 | tf_op jit(solution)/shard_map/psum | solution.py:34
  (6 shorter events, 0.1 us)
Async XLA Ops:
  7.2 92.8 %all-gather.5.cloned.1.call-start = ((), (), s32[]{:S(2)}) async-start(), calls=%async_computation.2 | async-start | bytes 7077888 | tf_op jit(solution)/shard_map/all_gather | solution.py:15
  26.2 163.5 %all-gather.3.cloned.1.call-start = ((), (), s32[]{:S(2)}) async-start(), calls=%async_computation.1 | async-start | bytes 18874368 | tf_op jit(solution)/shard_map/all_gather | solution.py:65
  208.0 2.7 copy-start
  208.0 3.0 %copy-start.1 = (s32[768]{0:T(1024)S(1)}, s32[768]{0:T(1024)}, u32[]{:S(2)}) copy-start(s32[768]{0:T(1024)} %param.5) | copy-start | bytes 9220
Sparse Core Ops, SparseCore 0:
  26.3 73.6 all-gather.4
  101.8 87.7 all-gather.2
where the time goes:
time: 282 us
  waiting for transfers between devices  163 us (58%)
  blocking collectives  76 us (27%)
  matrix products  18.3 us (6%)
  between operations  16 us (6%)
  other arithmetic  5.37 us (2%)
  local copies, waits for them, and re-layouts  3.03 us (1%)
    all_gather x1, waiting for transfers between devices, body(): lax.all_gather(out_embed, DP, axis=1, tiled=True)  89.7 us
    all_gather x1, waiting for transfers between devices, whole_of(): shard = lax.all_gather(shard, axis, axis=dim, tiled=True)  73 us
    psum x4, blocking collectives, one_axis_at_a_time(): shard = lax.psum(shard, axis)  38.5 us
    all_gather x1, blocking collectives, whole_of(): shard = lax.all_gather(shard, axis, axis=dim, tiled=True)  18.9 us
    all_to_all x1, blocking collectives, side_by_side(): lax.all_to_all(both, axis, split_axis=split_dim, concat_axis=concat_dim,...  18.5 us
    dot_general x1, matrix products, body(): lax.dot_general(lax.all_gather(out_embed, DP, axis=1, tiled=True), full_h...  18.3 us
  transfers between devices with their start and end apart: 2, of which 2 were waited for; matrix products, arithmetic and copies ran while one was open for 0% of the time, Pallas kernels for 0%

commit v1 on v0

--- a/solution.py
+++ b/solution.py
@@ -8,6 +8,13 @@
 TENSOR = ("tensor_0", "tensor_1")
 DP = ("dp_0", "dp_1")
 DP_TENSOR = ("dp_0", "dp_1", "tensor_0", "tensor_1")
+
+
+def swapped_in(block, mesh_axis, dim):
+    n_dev = lax.axis_size(mesh_axis)
+    shards = jnp.stack([block for _ in range(n_dev)])
+    shards = lax.all_to_all(shards, mesh_axis, split_axis=0, concat_axis=0)
+    return jnp.concatenate(shards, axis=dim)
 
 
 def whole_of(shard, axes, dim):
@@ -62,7 +69,7 @@
     vocab_offset = lax.axis_index(TENSOR) * vocab_rows
     block_count = vocab_rows // BLOCK
     all_logits = lax.dot_general(
-        lax.all_gather(out_embed, DP, axis=1, tiled=True),
+        swapped_in(out_embed, DP, 1),
         full_hidden,
         (((1,), (1,)), ((), ())),
         preferred_element_type=jnp.float32,

time: 282 us -> 300 us (1.064)
  local copies, waits for them, and re-layouts: 3.03 us -> 11.9 us
  starting transfers between devices: 0.08 us -> 5.93 us
  waiting for transfers between devices: 163 us -> 166 us
    all_to_all x0 -> x1, waiting for transfers between devices: none -> 91.6 us  [swapped_in(): shards = lax.all_to_all(shards, mesh_axis, split_axis=0, concat_axis=0)]
    all_gather x1 -> x0, waiting for transfers between devices: 89.7 us -> none  [body(): lax.all_gather(out_embed, DP, axis=1, tiled=True)]
    another operation x0 -> x1, local copies, waits for them, and re-layouts: none -> 5.98 us  [swapped_in(): shards = jnp.stack([block for _ in range(n_dev)])]
    all_to_all x0 -> x1, starting transfers between devices: none -> 5.89 us  [swapped_in(): shards = lax.all_to_all(shards, mesh_axis, split_axis=0, concat_axis=0)]
where the time goes in v1:
time: 300 us
  waiting for transfers between devices  166 us (55%)
  blocking collectives  76.2 us (25%)
  matrix products  18 us (6%)
  between operations  16 us (5%)
  local copies, waits for them, and re-layouts  11.9 us (4%)
  starting transfers between devices  5.93 us (2%)
  other arithmetic  5.37 us (2%)
    all_to_all x1, waiting for transfers between devices, swapped_in(): shards = lax.all_to_all(shards, mesh_axis, split_axis=0, concat_axis=0)  91.6 us
    all_gather x1, waiting for transfers between devices, whole_of(): shard = lax.all_gather(shard, axis, axis=dim, tiled=True)  74.6 us
    psum x4, blocking collectives, one_axis_at_a_time(): shard = lax.psum(shard, axis)  38.3 us
    all_to_all x1, blocking collectives, side_by_side(): lax.all_to_all(both, axis, split_axis=split_dim, concat_axis=concat_dim,...  19.7 us
    all_gather x1, blocking collectives, whole_of(): shard = lax.all_gather(shard, axis, axis=dim, tiled=True)  18.1 us
    dot_general x1, matrix products, body(): lax.dot_general(swapped_in(out_embed, DP, 1), full_hidden, (((1,), (1,)),...  18 us
  transfers between devices with their start and end apart: 2, of which 2 were waited for; matrix products, arithmetic and copies ran while one was open for 0% of the time, Pallas kernels for 0%

profile of v1, /device:TPU:32, one launch (start us, length us, event | category | flops | bytes accessed | tf_op | source)
XLA Modules:
  0.0 299.6 jit_solution(14374093533055395081)
XLA Ops:
  7.2 2.9 copy.6
  10.1 6.0 %stack.2 = bf16[8,2048,512]{1,2,0:T(8,128)(2,1)} broadcast(bf16[2048,512]{0,1:T(8,128)(2,1)S(1)} %copy.6), dimensions={1,2} | broadcast | bytes 18874368 | tf_op jit(solution)/shard_map/stack | solution.py:15
  16.1 0.0 copy-start.1
  16.1 5.9 %all-to-all-start = ((bf16[8,2048,512]{1,2,0:T(8,128)(2,1)}), bf16[8,2048,512]{1,2,0:T(8,128)(2,1)}, u32[]{:S(2)}, u32[]{:S(2)}) async-start(bf16[8,2048,512]{1,2,0:T(8,128)(2,1)} %stack.2), calls=%async_computation | async-start | bytes 33554432 | tf_op jit(solution)/shard_map/all_to_all | solution.py:16
  22.0 0.0 all-gather.2.cloned.1.call-start
  22.0 0.0 copy-done.1
  22.0 18.1 %all_gather.6 = bf16[768,512]{1,0:T(8,128)(2,1)} all-gather(bf16[768,128]{1,0:T(8,128)(2,1)S(1)} %copy-done.1), channel_id=1, replica_groups=mesh['dp_0'=4,'dp_1'=2,'tensor_0'=8,'tensor_1'=4] {'tensor_1'}, dimensions={1}, use_global_device_ids=true | all-gather | bytes 983040 | tf_op jit(solution)/shard_map/all_gather | solution.py:22
  40.2 0.0 all-gather.2.cloned.1.call-update
  40.2 74.6 %all-gather.2.cloned.1.call-done = bf16[768,4096]{1,0:T(8,128)(2,1)} async-done(((bf16[768,512]{1,0:T(8,128)(2,1)}), bf16[768,4096]{1,0:T(8,128)(2,1)}) %all-gather.2.cloned.1.call-update) | async-done | bytes 6291472 | tf_op jit(solution)/shard_map/all_gather | solution.py:22
  114.8 91.6 %all-to-all-done = bf16[8,2048,512]{1,2,0:T(8,128)(2,1)} async-done(((bf16[8,2048,512]{1,2,0:T(8,128)(2,1)}), bf16[8,2048,512]{1,2,0:T(8,128)(2,1)}, u32[]{:S(2)}, u32[]{:S(2)}) %all-to-all-start) | async-done | bytes 16777248 | tf_op jit(solution)/shard_map/all_to_all | solution.py:16
  206.4 18.0 %fusion.3 = f32[2048,768]{1,0:T(8,128)S(1)} fusion(bf16[2048,4096]{0,1:T(8,128)(2,1)} %bitcast.1, bf16[768,4096]{1,0:T(8,128)(2,1)} %all-gather.2.cloned.1.call-done), kind=kOutput, calls=%fused_computation.26 | convolution fusion | flops 12884901888 | bytes 29360128 | tf_op jit(solution)/shard_map/dot_general | solution.py:71
  224.4 0.0 copy-start
  224.4 0.0 copy-start.2
  224.4 0.3 slice_reduce_fusion.1
  224.8 2.3 copy-done
  227.1 0.1 reduce_max.60
  227.2 0.1 reduce_max.58
  227.3 0.1 reduce_max.54
  227.3 0.1 reduce_max.56
  227.4 0.0 copy-done.2
  227.4 3.7 %exponential_reduce_fusion.3 = (f32[768]{0:T(1024)S(1)}, f32[768]{0:T(1024)S(1)}, f32[768]{0:T(1024)S(1)}, f32[768]{0:T(1024)S(1)}, f32[768]{0:T(1024)S(1)}, /*i...) fusion(f32[2048,768]{1,0:T(8,128)} %copy-done, f32[768]{0:T(1024)S(1)} %get-tuple-element.17, ...), kind=kLoop, calls=%fused_computation.7 | loop fusion | flops 7858176 | bytes 6339584 | tf_op jit(solution)/shard_map/reduce_sum | solution.py:57
  231.1 0.1 add.98
  231.2 0.1 reduce_sum.114
  231.3 0.1 reduce_sum.112
  231.4 0.1 reduce_sum.110
  231.5 0.1 reduce_sum.108
  231.6 0.1 pad_maximum_fusion
  231.7 19.7 %all_to_all.17 = f32[32,1,72]{2,1,0:T(1,128)S(1)} all-to-all(f32[32,1,72]{2,1,0:T(1,128)S(1)} %bitcast.11), channel_id=1, replica_groups=mesh['dp_0'=4,'dp_1'=2,'tensor_0'=8,'tensor_1'=4] {'tensor_0','tensor_1'}, dimensions={0} | all-to-all | bytes 18432 | tf_op jit(solution)/shard_map/all_to_all | solution.py:29
  251.5 0.1 fusion
  251.5 1.1 fusion.1
  252.7 9.5 %psum.28 = f32[]{:T(128)} all-reduce(f32[]{:T(128)} %get-tuple-element.20), channel_id=1, replica_groups=mesh['dp_0'=4,'dp_1'=2,'tensor_0'=8,'tensor_1'=4] {'dp_0'}, use_global_device_ids=true, to_apply=%region_16.17 | all-reduce | flops 1 | bytes 8 | tf_op jit(solution)/shard_map/psum | solution.py:41
  262.2 3.1 %psum.29 = f32[]{:T(128)} all-reduce(f32[]{:T(128)} %psum.28), channel_id=1, replica_groups=mesh['dp_0'=4,'dp_1'=2,'tensor_0'=8,'tensor_1'=4] {'dp_1'}, use_global_device_ids=true, to_apply=%region_17.18 | all-reduce | flops 1 | bytes 8 | tf_op jit(solution)/shard_map/psum | solution.py:41
  265.2 16.2 %psum.30 = f32[]{:T(128)} all-reduce(f32[]{:T(128)} %psum.29), channel_id=1, replica_groups=mesh['dp_0'=4,'dp_1'=2,'tensor_0'=8,'tensor_1'=4] {'tensor_0'}, use_global_device_ids=true, to_apply=%region_18.19 | all-reduce | flops 1 | bytes 8 | tf_op jit(solution)/shard_map/psum | solution.py:41
  281.4 9.6 %psum.31 = f32[]{:T(128)} all-reduce(f32[]{:T(128)} %psum.30), channel_id=1, replica_groups=mesh['dp_0'=4,'dp_1'=2,'tensor_0'=8,'tensor_1'=4] {'tensor_1'}, use_global_device_ids=true, to_apply=%region_19.20 | all-reduce | flops 1 | bytes 8 | tf_op jit(solution)/shard_map/psum | solution.py:41
  (6 shorter events, 0.1 us)
Async XLA Ops:
  16.1 6.0 %copy-start.1 = (bf16[768,128]{1,0:T(8,128)(2,1)S(1)}, bf16[768,128]{1,0:T(8,128)(2,1)}, u32[]{:S(2)}) copy-start(bf16[768,128]{1,0:T(8,128)(2,1)} %param.3) | copy-start | bytes 589828
  16.1 190.4 %all-to-all-start = ((bf16[8,2048,512]{1,2,0:T(8,128)(2,1)}), bf16[8,2048,512]{1,2,0:T(8,128)(2,1)}, u32[]{:S(2)}, u32[]{:S(2)}) async-start(bf16[8,2048,512]{1,2,0:T(8,128)(2,1)} %stack.2), calls=%async_computation | async-start | bytes 33554432 | tf_op jit(solution)/shard_map/all_to_all | solution.py:16
  22.0 92.8 %all-gather.2.cloned.1.call-start = ((), (), s32[]{:S(2)}) async-start(), calls=%async_computation.2 | async-start | bytes 7077888 | tf_op jit(solution)/shard_map/all_gather | solution.py:22
  224.4 2.7 copy-start
  224.4 3.0 copy-start.2
Sparse Core Ops, SparseCore 0:
  40.3 74.4 all-gather.1
